TPU v7x, 32 devices: a whole 2x2x4 slice. The times are simulated.
32 devices in a mesh: gx: 4 (over z), gy: 2 (over x), gz: 4 (over y, core).
Axes of the slice: x: 2, y: 2, z: 4, core: 2. Of those that a mesh axis runs over, the one named last changes fastest.
Arguments:
- images: float32 [2, 64, 64, 512], P(None, 'gx', 'gy', 'gz'), may hold values from -6 to 6
- velocity: float32 [2, 3, 8, 8, 64], P(None, None, 'gx', None, 'gz'), may hold values from -2 to 2
Outputs:
- new_velocity: float32 [2, 3, 8, 8, 64], P(None, None, 'gx', None, 'gz')
- velocity_field: bfloat16 [2, 3, 64, 64, 512], P(None, None, 'gx', 'gy', 'gz')
All inputs are finite; a program needn't handle non-finite values.
Results may differ from a plain program's by a relative error of at most 0.001.
Values sent between devices are 32-bit elements; how exact they have to be, the bound alone decides.
A program may use at most 64 MiB of HBM per device.

v0:
```python
import jax
import jax.numpy as jnp
from jax import lax
from jax.sharding import PartitionSpec as P

epsilon_value = 1e-05
step_size = 0.5


def extended_2(cells, sides, width):
    for axis, dim in sides:
        count = lax.axis_size(axis)
        ends = count - 1
        head = lax.slice_in_dim(cells, 0, width, axis=dim)
        tail = lax.slice_in_dim(cells, cells.shape[dim] - width, cells.shape[dim], axis=dim)
        cells = jnp.concatenate(
            [
                lax.ppermute(tail, axis, [(i, (i + 1) % count) for i in range(ends)]),
                cells,
                lax.ppermute(head, axis, [((i + 1) % count, i) for i in range(ends)]),
            ],
            axis=dim,
        )
    return cells


def spline_weight(offset):
    magnitude = jnp.abs(offset)
    interior = 2.0 / 3.0 - magnitude * magnitude + 0.5 * magnitude * magnitude * magnitude
    outside = jnp.maximum(2.0 - magnitude, 0.0)
    outside = outside * outside * outside / 6.0
    return jnp.where(magnitude < 1.0, interior, outside)


def spline_table(voxels, points, first_point):
    positions = jnp.arange(voxels, dtype=jnp.float32)[:, None]
    centres = 8.0 * (jnp.arange(points, dtype=jnp.float32)[None, :] + first_point) + 3.5
    return spline_weight((positions - centres) / 8.0)


def fold_matrix(length):
    table_rows = jnp.arange(length, dtype=jnp.int32)[:, None]
    columns = jnp.arange(length - 8, dtype=jnp.int32)[None, :]
    matches = (
        (table_rows == columns + 4)
        | (table_rows < 2) & (columns == table_rows)
        | (table_rows >= length - 2) & (columns == table_rows - 8)
    )
    return matches.astype(jnp.float32)


def window_sum(values, which_axis, keep_count):
    running = lax.slice_in_dim(values, 0, keep_count, axis=which_axis)
    for offset in range(1, 9):
        running = running + lax.slice_in_dim(values, offset, offset + keep_count, axis=which_axis)
    return running


def gradient(volume, count_x, count_y, count_z):
    along_x = (
        volume[5 : 5 + count_x, 4 : 4 + count_y, 4 : 4 + count_z]
        - volume[3 : 3 + count_x, 4 : 4 + count_y, 4 : 4 + count_z]
    )
    along_y = (
        volume[4 : 4 + count_x, 5 : 5 + count_y, 4 : 4 + count_z]
        - volume[4 : 4 + count_x, 3 : 3 + count_y, 4 : 4 + count_z]
    )
    along_z = (
        volume[4 : 4 + count_x, 4 : 4 + count_y, 5 : 5 + count_z]
        - volume[4 : 4 + count_x, 4 : 4 + count_y, 3 : 3 + count_z]
    )
    return 0.5 * jnp.stack([along_x, along_y, along_z])


def local_forces(padded):
    count_x = padded.shape[1] - 8
    count_y = padded.shape[2] - 8
    count_z = padded.shape[3] - 8
    fixed_side = padded[0]
    moving_side = padded[1]
    products = jnp.stack(
        [
            fixed_side,
            moving_side,
            fixed_side * fixed_side,
            moving_side * moving_side,
            fixed_side * moving_side,
        ]
    )
    window_sums = window_sum(window_sum(window_sum(products, 1, count_x), 2, count_y), 3, count_z)
    averages = window_sums / 729.0
    mean_fixed = averages[0]
    mean_moving = averages[1]
    var_fixed = averages[2] - mean_fixed * mean_fixed + epsilon_value
    var_moving = averages[3] - mean_moving * mean_moving + epsilon_value
    covariance = averages[4] - mean_fixed * mean_moving
    centre_fixed = fixed_side[4 : 4 + count_x, 4 : 4 + count_y, 4 : 4 + count_z] - mean_fixed
    centre_moving = moving_side[4 : 4 + count_x, 4 : 4 + count_y, 4 : 4 + count_z] - mean_moving
    factor = 2.0 * covariance / (var_fixed * var_moving)
    pull_fixed = factor * (centre_moving - covariance / var_fixed * centre_fixed)
    pull_moving = factor * (centre_fixed - covariance / var_moving * centre_moving)
    return jnp.stack(
        [
            pull_fixed[None] * gradient(fixed_side, count_x, count_y, count_z),
            pull_moving[None] * gradient(moving_side, count_x, count_y, count_z),
        ]
    )


def shards(images, velocity):
    highest = lax.Precision.HIGHEST
    count_x = images.shape[1]
    count_y = images.shape[2]
    count_z = images.shape[3]
    block_x = count_x // 8
    block_y = count_y // 8
    block_z = count_z // 8
    padded = extended_2(images, (("gx", 1), ("gy", 2), ("gz", 3)), 4)
    pushes = local_forces(padded)
    table_x = spline_table(count_x, block_x + 4, -2.0)
    table_y = spline_table(count_y, block_y + 4, -2.0)
    table_z = spline_table(count_z, block_z + 4, -2.0)
    along_z = jnp.einsum("hcxyz,zk->hcxyk", pushes, table_z, precision=highest)
    along_y = jnp.einsum("hcxyk,yj->hcxjk", along_z, table_y, precision=highest)
    partial_value = jnp.einsum("hcxjk,xi->hcijk", along_y, table_x, precision=highest)
    fold_x = fold_matrix(block_x + 8)
    fold_z = fold_matrix(block_z + 8)
    extended = extended_2(partial_value, (("gx", 2), ("gz", 4)), 2)
    folded = jnp.einsum("hcpqr,pi->hciqr", extended, fold_x, precision=highest)
    folded = jnp.einsum("hciqr,rk->hciqk", folded, fold_z, precision=highest)
    whole_rows = block_y * lax.axis_size("gy") + 4
    canvas = jnp.zeros((2, 3, block_x, whole_rows, block_z), jnp.float32)
    canvas = lax.dynamic_update_slice_in_dim(canvas, folded, lax.axis_index("gy") * block_y, 3)
    summed = lax.psum(canvas, "gy")
    descent = summed[:, :, :, 2 : whole_rows - 2, :]
    new_velocity = velocity + step_size * descent
    beside_all = extended_2(new_velocity, (("gx", 2), ("gz", 4)), 2)
    rows_padded = jnp.pad(beside_all, ((0, 0), (0, 0), (0, 0), (2, 2), (0, 0)))
    window = lax.dynamic_slice_in_dim(rows_padded, lax.axis_index("gy") * block_y, block_y + 4, 3)
    field_x = jnp.einsum("hcijk,xi->hcxjk", window, table_x, precision=highest)
    field_y = jnp.einsum("hcxjk,yj->hcxyk", field_x, table_y, precision=highest)
    velocity_field = jnp.einsum("hcxyk,zk->hcxyz", field_y, table_z, precision=highest).astype(
        jnp.bfloat16
    )
    return (new_velocity, velocity_field)


def solution(mesh):
    placed = (P(None, "gx", "gy", "gz"), P(None, None, "gx", None, "gz"))
    return jax.shard_map(
        shards,
        mesh=mesh,
        in_specs=placed,
        out_specs=(P(None, None, "gx", None, "gz"), P(None, None, "gx", "gy", "gz")),
        check_vma=False,
    )
```

profile of v0, /device:TPU:1, one launch (start us, length us, event | category | flops | bytes accessed | tf_op | source)
XLA Modules:
  0.0 113.0 jit_solution(16727576706066880578)
XLA Ops:
  0.6 1.0 fusion.202
  1.6 4.0 %collective-permute-start = (f32[2,4,32,128]{3,2,1,0:T(8,128)S(1)}, f32[2,4,32,128]{3,2,1,0:T(8,128)S(1)}, u32[]{:S(2)}, u32[]{:S(2)}) collective-permute-start(f32[2,4,32,128]{3,2,1,0:T(8,128)S(1)} %get-tuple-element.25), channel_id=1, source_target_pairs={{0,8},{8,16},{16,24},{1,9},{9,17},{17,25},{2,10},{10,18},{18,26},{... | collective-permute-start | bytes 393224 | tf_op jit(solution)/shard_map/ppermute | solution.py:18
  5.7 1.3 %collective-permute-start.1 = (f32[2,4,32,128]{3,2,1,0:T(8,128)S(1)}, f32[2,4,32,128]{3,2,1,0:T(8,128)S(1)}, u32[]{:S(2)}, u32[]{:S(2)}) collective-permute-start(f32[2,4,32,128]{3,2,1,0:T(8,128)S(1)} %get-tuple-element.24), channel_id=1, source_target_pairs={{8,0},{16,8},{24,16},{9,1},{17,9},{25,17},{10,2},{18,10},{26,18},{... | collective-permute-start | bytes 393224 | tf_op jit(solution)/shard_map/ppermute | solution.py:20
  7.0 0.8 collective-permute-done
  7.8 1.1 constant_dynamic-update-slice_fusion.1
  8.9 2.5 %collective-permute-done.1 = f32[2,4,32,128]{3,2,1,0:T(8,128)S(1)} collective-permute-done((f32[2,4,32,128]{3,2,1,0:T(8,128)S(1)}, f32[2,4,32,128]{3,2,1,0:T(8,128)S(1)}, u32[]{:S(2)}, u32[]{:S(2)}) %collective-permute-start.1) | collective-permute-done | bytes 131104 | tf_op jit(solution)/shard_map/ppermute | solution.py:20
  11.4 3.1 %collective-permute-start.2 = (f32[2,24,4,128]{3,1,2,0:T(8,128)S(1)}, f32[2,24,4,128]{3,1,2,0:T(8,128)S(1)}, u32[]{:S(2)}, u32[]{:S(2)}) collective-permute-start(f32[2,24,4,128]{3,1,2,0:T(8,128)S(1)} %copy.59), channel_id=1, source_target_pairs={{0,4},{1,5},{2,6},{3,7},{8,12},{9,13},{10,14},{11,15},{16,20},{17,... | collective-permute-start | bytes 294920 | tf_op jit(solution)/shard_map/ppermute | solution.py:18
  14.6 1.3 %collective-permute-start.3 = (f32[2,24,4,128]{3,1,2,0:T(8,128)S(1)}, f32[2,24,4,128]{3,1,2,0:T(8,128)S(1)}, u32[]{:S(2)}, u32[]{:S(2)}) collective-permute-start(f32[2,24,4,128]{3,1,2,0:T(8,128)S(1)} %copy.60), channel_id=1, source_target_pairs={{4,0},{5,1},{6,2},{7,3},{12,8},{13,9},{14,10},{15,11},{20,16},{21,... | collective-permute-start | bytes 294920 | tf_op jit(solution)/shard_map/ppermute | solution.py:20
  15.9 0.3 collective-permute-done.2
  16.2 3.7 %collective-permute-done.3 = f32[2,24,4,128]{3,1,2,0:T(8,128)S(1)} collective-permute-done((f32[2,24,4,128]{3,1,2,0:T(8,128)S(1)}, f32[2,24,4,128]{3,1,2,0:T(8,128)S(1)}, u32[]{:S(2)}, u32[]{:S(2)}) %collective-permute-start.3) | collective-permute-done | bytes 98336 | tf_op jit(solution)/shard_map/ppermute | solution.py:20
  20.1 0.3 fusion.200
  20.4 0.4 copy.44
  20.8 6.6 %collective-permute-start.4 = (f32[2,24,40,4]{2,1,3,0:T(8,128)S(1)}, f32[2,24,40,4]{2,1,3,0:T(8,128)S(1)}, u32[]{:S(2)}, u32[]{:S(2)}) collective-permute-start(f32[2,24,40,4]{2,1,3,0:T(8,128)S(1)} %copy.44), channel_id=1, source_target_pairs={{0,1},{1,2},{2,3},{4,5},{5,6},{6,7},{8,9},{9,10},{10,11},{12,13},{... | collective-permute-start | bytes 92168 | tf_op jit(solution)/shard_map/ppermute | solution.py:18
  27.4 0.4 copy.45
  27.8 1.9 %collective-permute-start.5 = (f32[2,24,40,4]{2,1,3,0:T(8,128)S(1)}, f32[2,24,40,4]{2,1,3,0:T(8,128)S(1)}, u32[]{:S(2)}, u32[]{:S(2)}) collective-permute-start(f32[2,24,40,4]{2,1,3,0:T(8,128)S(1)} %copy.45), channel_id=1, source_target_pairs={{1,0},{2,1},{3,2},{5,4},{6,5},{7,6},{9,8},{10,9},{11,10},{13,12},{... | collective-permute-start | bytes 92168 | tf_op jit(solution)/shard_map/ppermute | solution.py:20
  29.8 0.4 copy.46
  30.2 3.6 %collective-permute-done.5 = f32[2,24,40,4]{2,1,3,0:T(8,128)S(1)} collective-permute-done((f32[2,24,40,4]{2,1,3,0:T(8,128)S(1)}, f32[2,24,40,4]{2,1,3,0:T(8,128)S(1)}, u32[]{:S(2)}, u32[]{:S(2)}) %collective-permute-start.5) | collective-permute-done | bytes 30752 | tf_op jit(solution)/shard_map/ppermute | solution.py:20
  33.7 0.4 copy.47
  34.2 1.0 pad_maximum_fusion.1
  35.2 0.4 slice_bitcast_fusion.1
  35.6 1.8 %pad_maximum_fusion = f32[5,24,40,136]{3,2,1,0:T(8,128)S(1)} fusion(f32[1,24,40,136]{3,2,1,0:T(8,128)S(1)} %get-tuple-element.12, f32[1,24,40,136]{3,2,1,0:T(8,128)S(1)} %get-tuple-element.14, f32[1,24,40,136]{3,2,1,0:T(8,128)S(1)} %get-tuple-element.11, f32[2,24,40,4]{3,2,1,0:T(8,128)S(1)} %copy.47, f32[2,24,4,128]{3,2,1,0:T(4,128)S(1)} %copy.43, ...), kind=kLoop, calls=%fused_computation | loop fusion | flops 4569600 | bytes 5222400 | tf_op jit(solution)/shard_map/stack | solution.py:81
  37.4 3.0 %slice_add_fusion = f32[5,16,40,136]{3,2,1,0:T(8,128)S(1)} fusion(f32[5,24,40,136]{3,2,1,0:T(8,128)S(1)} %pad_maximum_fusion), kind=kLoop, calls=%fused_computation.1 | loop fusion | flops 3481600 | bytes 17408000 | tf_op jit(solution)/shard_map/add | solution.py:55
  40.5 2.0 %slice_add_fusion.8 = f32[5,16,32,136]{3,2,1,0:T(8,128)S(1)} fusion(f32[5,16,40,136]{3,2,1,0:T(8,128)S(1)} %slice_add_fusion), kind=kLoop, calls=%fused_computation.9 | loop fusion | flops 2785280 | bytes 13926400 | tf_op jit(solution)/shard_map/add | solution.py:55
  42.4 2.8 %fusion.4 = f32[5,16,32,128]{3,2,1,0:T(8,128)S(1)} fusion(f32[5,16,32,136]{3,2,1,0:T(8,128)S(1)} %slice_add_fusion.8), kind=kLoop, calls=%fused_computation.25 | loop fusion | flops 2949120 | bytes 13107200 | tf_op jit(solution)/shard_map/div | solution.py:91
  45.2 0.6 fusion.18
  45.8 0.5 multiply_multiply_fusion.1
  46.5 6.2 %fusion = f32[2,3,16,32,20]{3,4,2,1,0:T(8,128)S(1)} fusion(f32[1,3,16,32,128]{4,3,2,1,0:T(8,128)S(1)} %maximum_multiply_fusion.1, f32[1,3,16,32,128]{4,3,2,1,0:T(8,128)S(1)} %maximum_multiply_fusion, f32[20]{0:T(128)S(1)} %multiply_add_fusion), kind=kOutput, calls=%fused_computation.18 | convolution fusion | flops 94806016 | bytes 1818704 | tf_op jit(solution)/shard_map/hcxyz,zk->hcxyk/dot_general | solution.py:123
  52.7 5.9 %convolution_bitcast_fusion.2 = f32[2,3,16,8,20]{4,3,2,1,0:T(8,128)S(1)} fusion(f32[2,3,16,32,20]{3,4,2,1,0:T(8,128)S(1)} %fusion, f32[8]{0:T(128)S(1)} %multiply_add_fusion.1), kind=kOutput, calls=%fused_computation.34 | convolution fusion | flops 5902336 | bytes 307232 | tf_op jit(solution)/shard_map/hcxyk,yj->hcxjk/dot_general | solution.py:124
  58.6 0.4 convolution_bitcast_fusion.3
  59.1 3.2 %collective-permute-start.6 = (f32[2,3,2,8,20]{4,2,3,1,0:T(2,128)S(1)}, f32[2,3,2,8,20]{4,2,3,1,0:T(2,128)S(1)}, u32[]{:S(2)}, u32[]{:S(2)}) collective-permute-start(f32[2,3,2,8,20]{4,2,3,1,0:T(2,128)S(1)} %get-tuple-element.30), channel_id=1, source_target_pairs={{0,8},{8,16},{16,24},{1,9},{9,17},{17,25},{2,10},{10,18},{18,26},{... | collective-permute-start | bytes 23048 | tf_op jit(solution)/shard_map/ppermute | solution.py:18
  62.3 1.5 %collective-permute-start.7 = (f32[2,3,2,8,20]{4,2,3,1,0:T(2,128)S(1)}, f32[2,3,2,8,20]{4,2,3,1,0:T(2,128)S(1)}, u32[]{:S(2)}, u32[]{:S(2)}) collective-permute-start(f32[2,3,2,8,20]{4,2,3,1,0:T(2,128)S(1)} %get-tuple-element.31), channel_id=1, source_target_pairs={{8,0},{16,8},{24,16},{9,1},{17,9},{25,17},{10,2},{18,10},{26,18},{... | collective-permute-start | bytes 23048 | tf_op jit(solution)/shard_map/ppermute | solution.py:20
  63.8 3.3 %collective-permute-done.7 = f32[2,3,2,8,20]{4,2,3,1,0:T(2,128)S(1)} collective-permute-done((f32[2,3,2,8,20]{4,2,3,1,0:T(2,128)S(1)}, f32[2,3,2,8,20]{4,2,3,1,0:T(2,128)S(1)}, u32[]{:S(2)}, u32[]{:S(2)}) %collective-permute-start.7) | collective-permute-done | bytes 7712 | tf_op jit(solution)/shard_map/ppermute | solution.py:20
  67.4 3.3 %collective-permute-start.8 = (f32[2,3,10,8,2]{4,2,3,1,0:T(8,128)S(1)}, f32[2,3,10,8,2]{4,2,3,1,0:T(8,128)S(1)}, u32[]{:S(2)}, u32[]{:S(2)}) collective-permute-start(f32[2,3,10,8,2]{4,2,3,1,0:T(8,128)S(1)} %get-tuple-element.26), channel_id=1, source_target_pairs={{0,1},{1,2},{2,3},{4,5},{5,6},{6,7},{8,9},{9,10},{10,11},{12,13},{... | collective-permute-start | bytes 11528 | tf_op jit(solution)/shard_map/ppermute | solution.py:18
  70.6 1.9 %collective-permute-start.9 = (f32[2,3,10,8,2]{4,2,3,1,0:T(8,128)S(1)}, f32[2,3,10,8,2]{4,2,3,1,0:T(8,128)S(1)}, u32[]{:S(2)}, u32[]{:S(2)}) collective-permute-start(f32[2,3,10,8,2]{4,2,3,1,0:T(8,128)S(1)} %get-tuple-element.27), channel_id=1, source_target_pairs={{1,0},{2,1},{3,2},{5,4},{6,5},{7,6},{9,8},{10,9},{11,10},{13,12},{... | collective-permute-start | bytes 11528 | tf_op jit(solution)/shard_map/ppermute | solution.py:20
  72.6 2.8 %collective-permute-done.8 = f32[2,3,10,8,2]{4,2,3,1,0:T(8,128)S(1)} collective-permute-done((f32[2,3,10,8,2]{4,2,3,1,0:T(8,128)S(1)}, f32[2,3,10,8,2]{4,2,3,1,0:T(8,128)S(1)}, u32[]{:S(2)}, u32[]{:S(2)}) %collective-permute-start.8) | collective-permute-done | bytes 3872 | tf_op jit(solution)/shard_map/ppermute | solution.py:18
  75.3 4.7 %collective-permute-done.9 = f32[2,3,10,8,2]{4,2,3,1,0:T(8,128)S(1)} collective-permute-done((f32[2,3,10,8,2]{4,2,3,1,0:T(8,128)S(1)}, f32[2,3,10,8,2]{4,2,3,1,0:T(8,128)S(1)}, u32[]{:S(2)}, u32[]{:S(2)}) %collective-permute-start.9) | collective-permute-done | bytes 3872 | tf_op jit(solution)/shard_map/ppermute | solution.py:20
  80.0 0.6 convolution_bitcast_fusion.4
  80.9 5.6 %psum.7 = f32[2,3,2,12,16]{4,2,3,1,0:T(2,128)S(1)} all-reduce(f32[2,3,2,12,16]{4,2,3,1,0:T(2,128)S(1)} %copy_dynamic-update-slice_fusion), channel_id=1, replica_groups=mesh['gx'=4,'gy'=2,'gz'=4] {'gy'}, use_global_device_ids=true, to_apply=%region_0.1 | all-reduce | flops 2304 | bytes 18432 | tf_op jit(solution)/shard_map/psum | solution.py:134
  86.6 3.2 %collective-permute-start.10 = (f32[2,3,2,8,16]{4,2,3,1,0:T(2,128)S(1)}, f32[2,3,2,8,16]{4,2,3,1,0:T(2,128)S(1)}, u32[]{:S(2)}, u32[]{:S(2)}) collective-permute-start(f32[2,3,2,8,16]{4,2,3,1,0:T(2,128)S(1)} %fusion.51), channel_id=1, source_target_pairs={{0,8},{8,16},{16,24},{1,9},{9,17},{17,25},{2,10},{10,18},{18,26},{... | collective-permute-start | bytes 18440 | tf_op jit(solution)/shard_map/ppermute | solution.py:18
  89.8 1.3 %collective-permute-start.11 = (f32[2,3,2,8,16]{4,2,3,1,0:T(2,128)S(1)}, f32[2,3,2,8,16]{4,2,3,1,0:T(2,128)S(1)}, u32[]{:S(2)}, u32[]{:S(2)}) collective-permute-start(f32[2,3,2,8,16]{4,2,3,1,0:T(2,128)S(1)} %fusion.51), channel_id=1, source_target_pairs={{8,0},{16,8},{24,16},{9,1},{17,9},{25,17},{10,2},{18,10},{26,18},{... | collective-permute-start | bytes 18440 | tf_op jit(solution)/shard_map/ppermute | solution.py:20
  91.1 3.5 %collective-permute-done.11 = f32[2,3,2,8,16]{4,2,3,1,0:T(2,128)S(1)} collective-permute-done((f32[2,3,2,8,16]{4,2,3,1,0:T(2,128)S(1)}, f32[2,3,2,8,16]{4,2,3,1,0:T(2,128)S(1)}, u32[]{:S(2)}, u32[]{:S(2)}) %collective-permute-start.11) | collective-permute-done | bytes 6176 | tf_op jit(solution)/shard_map/ppermute | solution.py:20
  94.8 4.6 %collective-permute-start.12 = (f32[2,3,6,8,2]{4,2,3,1,0:T(8,128)S(1)}, f32[2,3,6,8,2]{4,2,3,1,0:T(8,128)S(1)}, u32[]{:S(2)}, u32[]{:S(2)}) collective-permute-start(f32[2,3,6,8,2]{4,2,3,1,0:T(8,128)S(1)} %get-tuple-element.29), channel_id=1, source_target_pairs={{0,1},{1,2},{2,3},{4,5},{5,6},{6,7},{8,9},{9,10},{10,11},{12,13},{... | collective-permute-start | bytes 6920 | tf_op jit(solution)/shard_map/ppermute | solution.py:18
  99.4 1.9 %collective-permute-start.13 = (f32[2,3,6,8,2]{4,2,3,1,0:T(8,128)S(1)}, f32[2,3,6,8,2]{4,2,3,1,0:T(8,128)S(1)}, u32[]{:S(2)}, u32[]{:S(2)}) collective-permute-start(f32[2,3,6,8,2]{4,2,3,1,0:T(8,128)S(1)} %get-tuple-element.28), channel_id=1, source_target_pairs={{1,0},{2,1},{3,2},{5,4},{6,5},{7,6},{9,8},{10,9},{11,10},{13,12},{... | collective-permute-start | bytes 6920 | tf_op jit(solution)/shard_map/ppermute | solution.py:20
  101.4 0.6 copy.53
  102.0 4.4 %collective-permute-done.13 = f32[2,3,6,8,2]{4,2,3,1,0:T(8,128)S(1)} collective-permute-done((f32[2,3,6,8,2]{4,2,3,1,0:T(8,128)S(1)}, f32[2,3,6,8,2]{4,2,3,1,0:T(8,128)S(1)}, u32[]{:S(2)}, u32[]{:S(2)}) %collective-permute-start.13) | collective-permute-done | bytes 2336 | tf_op jit(solution)/shard_map/ppermute | solution.py:20
  106.4 0.9 convolution_bitcast_fusion.1
  107.4 2.1 %convolution_bitcast_fusion = f32[2,3,16,32,20]{3,4,2,1,0:T(8,128)S(1)} fusion(f32[2,3,16,8,20]{4,2,3,1,0:T(8,128)S(1)} %convolution_bitcast_fusion.1, f32[8]{0:T(128)S(1)} %multiply_add_fusion.1), kind=kOutput, calls=%fused_computation.23 | convolution fusion | flops 5902336 | bytes 307232 | tf_op jit(solution)/shard_map/hcxjk,yj->hcxyk/dot_general | solution.py:141
  109.4 3.6 %convolution_convert_fusion = bf16[2,3,16,32,128]{4,3,2,1,0:T(8,128)(2,1)} fusion(f32[2,3,16,32,20]{3,4,2,1,0:T(8,128)S(1)} %convolution_bitcast_fusion, f32[20]{0:T(128)S(1)} %multiply_add_fusion), kind=kOutput, calls=%fused_computation.22 | convolution fusion | flops 94806016 | bytes 1032272 | tf_op jit(solution)/shard_map/hcxyk,zk->hcxyz/dot_general | solution.py:142
  (35 shorter events, 1.4 us)
Async XLA Ops:
  1.6 6.2 %collective-permute-start = (f32[2,4,32,128]{3,2,1,0:T(8,128)S(1)}, f32[2,4,32,128]{3,2,1,0:T(8,128)S(1)}, u32[]{:S(2)}, u32[]{:S(2)}) collective-permute-start(f32[2,4,32,128]{3,2,1,0:T(8,128)S(1)} %get-tuple-element.25), channel_id=1, source_target_pairs={{0,8},{8,16},{16,24},{1,9},{9,17},{17,25},{2,10},{10,18},{18,26},{... | collective-permute-start | bytes 393224 | tf_op jit(solution)/shard_map/ppermute | solution.py:18
  5.7 5.7 %collective-permute-start.1 = (f32[2,4,32,128]{3,2,1,0:T(8,128)S(1)}, f32[2,4,32,128]{3,2,1,0:T(8,128)S(1)}, u32[]{:S(2)}, u32[]{:S(2)}) collective-permute-start(f32[2,4,32,128]{3,2,1,0:T(8,128)S(1)} %get-tuple-element.24), channel_id=1, source_target_pairs={{8,0},{16,8},{24,16},{9,1},{17,9},{25,17},{10,2},{18,10},{26,18},{... | collective-permute-start | bytes 393224 | tf_op jit(solution)/shard_map/ppermute | solution.py:20
  11.4 4.7 %collective-permute-start.2 = (f32[2,24,4,128]{3,1,2,0:T(8,128)S(1)}, f32[2,24,4,128]{3,1,2,0:T(8,128)S(1)}, u32[]{:S(2)}, u32[]{:S(2)}) collective-permute-start(f32[2,24,4,128]{3,1,2,0:T(8,128)S(1)} %copy.59), channel_id=1, source_target_pairs={{0,4},{1,5},{2,6},{3,7},{8,12},{9,13},{10,14},{11,15},{16,20},{17,... | collective-permute-start | bytes 294920 | tf_op jit(solution)/shard_map/ppermute | solution.py:18
  14.6 5.4 %collective-permute-start.3 = (f32[2,24,4,128]{3,1,2,0:T(8,128)S(1)}, f32[2,24,4,128]{3,1,2,0:T(8,128)S(1)}, u32[]{:S(2)}, u32[]{:S(2)}) collective-permute-start(f32[2,24,4,128]{3,1,2,0:T(8,128)S(1)} %copy.60), channel_id=1, source_target_pairs={{4,0},{5,1},{6,2},{7,3},{12,8},{13,9},{14,10},{15,11},{20,16},{21,... | collective-permute-start | bytes 294920 | tf_op jit(solution)/shard_map/ppermute | solution.py:20
  20.8 8.9 %collective-permute-start.4 = (f32[2,24,40,4]{2,1,3,0:T(8,128)S(1)}, f32[2,24,40,4]{2,1,3,0:T(8,128)S(1)}, u32[]{:S(2)}, u32[]{:S(2)}) collective-permute-start(f32[2,24,40,4]{2,1,3,0:T(8,128)S(1)} %copy.44), channel_id=1, source_target_pairs={{0,1},{1,2},{2,3},{4,5},{5,6},{6,7},{8,9},{9,10},{10,11},{12,13},{... | collective-permute-start | bytes 92168 | tf_op jit(solution)/shard_map/ppermute | solution.py:18
  27.8 5.9 %collective-permute-start.5 = (f32[2,24,40,4]{2,1,3,0:T(8,128)S(1)}, f32[2,24,40,4]{2,1,3,0:T(8,128)S(1)}, u32[]{:S(2)}, u32[]{:S(2)}) collective-permute-start(f32[2,24,40,4]{2,1,3,0:T(8,128)S(1)} %copy.45), channel_id=1, source_target_pairs={{1,0},{2,1},{3,2},{5,4},{6,5},{7,6},{9,8},{10,9},{11,10},{13,12},{... | collective-permute-start | bytes 92168 | tf_op jit(solution)/shard_map/ppermute | solution.py:20
  58.6 27.9 %copy-start = (f32[2,3,2,8,16]{4,3,2,1,0:T(8,128)S(1)}, f32[2,3,2,8,16]{4,3,2,1,0:T(8,128)}, u32[]{:S(2)}) copy-start(f32[2,3,2,8,16]{4,3,2,1,0:T(8,128)} %param.3) | copy-start | bytes 18436
  59.1 4.7 %collective-permute-start.6 = (f32[2,3,2,8,20]{4,2,3,1,0:T(2,128)S(1)}, f32[2,3,2,8,20]{4,2,3,1,0:T(2,128)S(1)}, u32[]{:S(2)}, u32[]{:S(2)}) collective-permute-start(f32[2,3,2,8,20]{4,2,3,1,0:T(2,128)S(1)} %get-tuple-element.30), channel_id=1, source_target_pairs={{0,8},{8,16},{16,24},{1,9},{9,17},{17,25},{2,10},{10,18},{18,26},{... | collective-permute-start | bytes 23048 | tf_op jit(solution)/shard_map/ppermute | solution.py:18
  62.3 4.8 %collective-permute-start.7 = (f32[2,3,2,8,20]{4,2,3,1,0:T(2,128)S(1)}, f32[2,3,2,8,20]{4,2,3,1,0:T(2,128)S(1)}, u32[]{:S(2)}, u32[]{:S(2)}) collective-permute-start(f32[2,3,2,8,20]{4,2,3,1,0:T(2,128)S(1)} %get-tuple-element.31), channel_id=1, source_target_pairs={{8,0},{16,8},{24,16},{9,1},{17,9},{25,17},{10,2},{18,10},{26,18},{... | collective-permute-start | bytes 23048 | tf_op jit(solution)/shard_map/ppermute | solution.py:20
  67.4 8.0 %collective-permute-start.8 = (f32[2,3,10,8,2]{4,2,3,1,0:T(8,128)S(1)}, f32[2,3,10,8,2]{4,2,3,1,0:T(8,128)S(1)}, u32[]{:S(2)}, u32[]{:S(2)}) collective-permute-start(f32[2,3,10,8,2]{4,2,3,1,0:T(8,128)S(1)} %get-tuple-element.26), channel_id=1, source_target_pairs={{0,1},{1,2},{2,3},{4,5},{5,6},{6,7},{8,9},{9,10},{10,11},{12,13},{... | collective-permute-start | bytes 11528 | tf_op jit(solution)/shard_map/ppermute | solution.py:18
  70.6 9.4 %collective-permute-start.9 = (f32[2,3,10,8,2]{4,2,3,1,0:T(8,128)S(1)}, f32[2,3,10,8,2]{4,2,3,1,0:T(8,128)S(1)}, u32[]{:S(2)}, u32[]{:S(2)}) collective-permute-start(f32[2,3,10,8,2]{4,2,3,1,0:T(8,128)S(1)} %get-tuple-element.27), channel_id=1, source_target_pairs={{1,0},{2,1},{3,2},{5,4},{6,5},{7,6},{9,8},{10,9},{11,10},{13,12},{... | collective-permute-start | bytes 11528 | tf_op jit(solution)/shard_map/ppermute | solution.py:20
  86.6 4.5 %collective-permute-start.10 = (f32[2,3,2,8,16]{4,2,3,1,0:T(2,128)S(1)}, f32[2,3,2,8,16]{4,2,3,1,0:T(2,128)S(1)}, u32[]{:S(2)}, u32[]{:S(2)}) collective-permute-start(f32[2,3,2,8,16]{4,2,3,1,0:T(2,128)S(1)} %fusion.51), channel_id=1, source_target_pairs={{0,8},{8,16},{16,24},{1,9},{9,17},{17,25},{2,10},{10,18},{18,26},{... | collective-permute-start | bytes 18440 | tf_op jit(solution)/shard_map/ppermute | solution.py:18
  89.8 4.8 %collective-permute-start.11 = (f32[2,3,2,8,16]{4,2,3,1,0:T(2,128)S(1)}, f32[2,3,2,8,16]{4,2,3,1,0:T(2,128)S(1)}, u32[]{:S(2)}, u32[]{:S(2)}) collective-permute-start(f32[2,3,2,8,16]{4,2,3,1,0:T(2,128)S(1)} %fusion.51), channel_id=1, source_target_pairs={{8,0},{16,8},{24,16},{9,1},{17,9},{25,17},{10,2},{18,10},{26,18},{... | collective-permute-start | bytes 18440 | tf_op jit(solution)/shard_map/ppermute | solution.py:20
  94.8 7.2 %collective-permute-start.12 = (f32[2,3,6,8,2]{4,2,3,1,0:T(8,128)S(1)}, f32[2,3,6,8,2]{4,2,3,1,0:T(8,128)S(1)}, u32[]{:S(2)}, u32[]{:S(2)}) collective-permute-start(f32[2,3,6,8,2]{4,2,3,1,0:T(8,128)S(1)} %get-tuple-element.29), channel_id=1, source_target_pairs={{0,1},{1,2},{2,3},{4,5},{5,6},{6,7},{8,9},{9,10},{10,11},{12,13},{... | collective-permute-start | bytes 6920 | tf_op jit(solution)/shard_map/ppermute | solution.py:18
  99.4 7.0 %collective-permute-start.13 = (f32[2,3,6,8,2]{4,2,3,1,0:T(8,128)S(1)}, f32[2,3,6,8,2]{4,2,3,1,0:T(8,128)S(1)}, u32[]{:S(2)}, u32[]{:S(2)}) collective-permute-start(f32[2,3,6,8,2]{4,2,3,1,0:T(8,128)S(1)} %get-tuple-element.28), channel_id=1, source_target_pairs={{1,0},{2,1},{3,2},{5,4},{6,5},{7,6},{9,8},{10,9},{11,10},{13,12},{... | collective-permute-start | bytes 6920 | tf_op jit(solution)/shard_map/ppermute | solution.py:20
where the time goes:
time: 114 us; the launch traced here: 113 us
  starting transfers between devices  39.2 us (34%)
  waiting for transfers between devices  29.5 us (26%)
  matrix products  19.8 us (17%)
  other arithmetic  12.7 us (11%)
  blocking collectives  5.6 us (5%)
  local copies, waits for them, and re-layouts  5.12 us (4%)
    ppermute x7, starting transfers between devices, extended_2(): lax.ppermute(tail, axis, [(i, (i + 1) % count) for i in range(ends)])  28 us
    ppermute x7, waiting for transfers between devices, extended_2(): lax.ppermute(head, axis, [((i + 1) % count, i) for i in range(ends)])  25.7 us
    ppermute x7, starting transfers between devices, extended_2(): lax.ppermute(head, axis, [((i + 1) % count, i) for i in range(ends)])  11.2 us
    dot_general x1, matrix products, shards(): along_z = jnp.einsum('hcxyz,zk->hcxyk', pushes, table_z, precision=highest)  6.22 us
    dot_general x1, matrix products, shards(): along_y = jnp.einsum('hcxyk,yj->hcxjk', along_z, table_y, precision=highest)  5.91 us
    psum x1, blocking collectives, shards(): summed = lax.psum(canvas, 'gy')  5.6 us
    add x2, other arithmetic, window_sum(): running + lax.slice_in_dim(values, offset, offset + keep_count, axis=whic...  5 us
    ppermute x7, waiting for transfers between devices, extended_2(): lax.ppermute(tail, axis, [(i, (i + 1) % count) for i in range(ends)])  3.85 us
  transfers between devices with their start and end apart: 14, of which 10 were waited for; matrix products, arithmetic and copies ran while one was open for 2% of the time, Pallas kernels for 0%

commit v1 on v0

--- a/solution.py
+++ b/solution.py
@@ -5,6 +5,10 @@
 
 epsilon_value = 1e-05
 step_size = 0.5
+
+
+def _do_rounds(row_data):
+    return lax.all_gather(row_data, "gy").sum(axis=0)
 
 
 def extended_2(cells, sides, width):
@@ -131,7 +135,7 @@
     whole_rows = block_y * lax.axis_size("gy") + 4
     canvas = jnp.zeros((2, 3, block_x, whole_rows, block_z), jnp.float32)
     canvas = lax.dynamic_update_slice_in_dim(canvas, folded, lax.axis_index("gy") * block_y, 3)
-    summed = lax.psum(canvas, "gy")
+    summed = _do_rounds(canvas)
     descent = summed[:, :, :, 2 : whole_rows - 2, :]
     new_velocity = velocity + step_size * descent
     beside_all = extended_2(new_velocity, (("gx", 2), ("gz", 4)), 2)

time: 114 us -> 111 us (0.974)
  blocking collectives: 5.6 us -> 3.87 us
    psum x1 -> x0, blocking collectives: 5.6 us -> none  [shards(): summed = lax.psum(canvas, 'gy')]
    all_gather x0 -> x1, blocking collectives: none -> 3.87 us  [_do_rounds(): return lax.all_gather(row_data, 'gy').sum(axis=0)]
where the time goes in v1:
time: 111 us
  starting transfers between devices  38.9 us (35%)
  waiting for transfers between devices  29.2 us (26%)
  matrix products  19.8 us (18%)
  other arithmetic  12.8 us (12%)
  local copies, waits for them, and re-layouts  5.12 us (5%)
  blocking collectives  3.87 us (3%)
    ppermute x7, starting transfers between devices, extended_2(): lax.ppermute(tail, axis, [(i, (i + 1) % count) for i in range(ends)])  27.7 us
    ppermute x7, waiting for transfers between devices, extended_2(): lax.ppermute(head, axis, [((i + 1) % count, i) for i in range(ends)])  25.4 us
    ppermute x7, starting transfers between devices, extended_2(): lax.ppermute(head, axis, [((i + 1) % count, i) for i in range(ends)])  11.2 us
    dot_general x1, matrix products, shards(): along_z = jnp.einsum('hcxyz,zk->hcxyk', pushes, table_z, precision=highest)  6.22 us
    dot_general x1, matrix products, shards(): along_y = jnp.einsum('hcxyk,yj->hcxjk', along_z, table_y, precision=highest)  5.91 us
    add x2, other arithmetic, window_sum(): running + lax.slice_in_dim(values, offset, offset + keep_count, axis=whic...  5 us
    all_gather x1, blocking collectives, _do_rounds(): return lax.all_gather(row_data, 'gy').sum(axis=0)  3.87 us
    ppermute x7, waiting for transfers between devices, extended_2(): lax.ppermute(tail, axis, [(i, (i + 1) % count) for i in range(ends)])  3.85 us
  transfers between devices with their start and end apart: 14, of which 10 were waited for; matrix products, arithmetic and copies ran while one was open for 2% of the time, Pallas kernels for 0%

profile of v1, /device:TPU:1, one launch (start us, length us, event | category | flops | bytes accessed | tf_op | source)
XLA Modules:
  0.0 110.8 jit_solution(423475223439617473)
XLA Ops:
  0.6 1.0 fusion.201
  1.6 4.0 %collective-permute-start = (f32[2,4,32,128]{3,2,1,0:T(8,128)S(1)}, f32[2,4,32,128]{3,2,1,0:T(8,128)S(1)}, u32[]{:S(2)}, u32[]{:S(2)}) collective-permute-start(f32[2,4,32,128]{3,2,1,0:T(8,128)S(1)} %get-tuple-element.25), channel_id=1, source_target_pairs={{0,8},{8,16},{16,24},{1,9},{9,17},{17,25},{2,10},{10,18},{18,26},{... | collective-permute-start | bytes 393224 | tf_op jit(solution)/shard_map/ppermute | solution.py:22
  5.7 1.3 %collective-permute-start.1 = (f32[2,4,32,128]{3,2,1,0:T(8,128)S(1)}, f32[2,4,32,128]{3,2,1,0:T(8,128)S(1)}, u32[]{:S(2)}, u32[]{:S(2)}) collective-permute-start(f32[2,4,32,128]{3,2,1,0:T(8,128)S(1)} %get-tuple-element.24), channel_id=1, source_target_pairs={{8,0},{16,8},{24,16},{9,1},{17,9},{25,17},{10,2},{18,10},{26,18},{... | collective-permute-start | bytes 393224 | tf_op jit(solution)/shard_map/ppermute | solution.py:24
  7.0 0.8 collective-permute-done
  7.8 1.1 constant_dynamic-update-slice_fusion.1
  8.9 2.5 %collective-permute-done.1 = f32[2,4,32,128]{3,2,1,0:T(8,128)S(1)} collective-permute-done((f32[2,4,32,128]{3,2,1,0:T(8,128)S(1)}, f32[2,4,32,128]{3,2,1,0:T(8,128)S(1)}, u32[]{:S(2)}, u32[]{:S(2)}) %collective-permute-start.1) | collective-permute-done | bytes 131104 | tf_op jit(solution)/shard_map/ppermute | solution.py:24
  11.4 3.1 %collective-permute-start.2 = (f32[2,24,4,128]{3,1,2,0:T(8,128)S(1)}, f32[2,24,4,128]{3,1,2,0:T(8,128)S(1)}, u32[]{:S(2)}, u32[]{:S(2)}) collective-permute-start(f32[2,24,4,128]{3,1,2,0:T(8,128)S(1)} %copy.60), channel_id=1, source_target_pairs={{0,4},{1,5},{2,6},{3,7},{8,12},{9,13},{10,14},{11,15},{16,20},{17,... | collective-permute-start | bytes 294920 | tf_op jit(solution)/shard_map/ppermute | solution.py:22
  14.6 1.3 %collective-permute-start.3 = (f32[2,24,4,128]{3,1,2,0:T(8,128)S(1)}, f32[2,24,4,128]{3,1,2,0:T(8,128)S(1)}, u32[]{:S(2)}, u32[]{:S(2)}) collective-permute-start(f32[2,24,4,128]{3,1,2,0:T(8,128)S(1)} %copy.61), channel_id=1, source_target_pairs={{4,0},{5,1},{6,2},{7,3},{12,8},{13,9},{14,10},{15,11},{20,16},{21,... | collective-permute-start | bytes 294920 | tf_op jit(solution)/shard_map/ppermute | solution.py:24
  15.9 0.3 collective-permute-done.2
  16.2 3.7 %collective-permute-done.3 = f32[2,24,4,128]{3,1,2,0:T(8,128)S(1)} collective-permute-done((f32[2,24,4,128]{3,1,2,0:T(8,128)S(1)}, f32[2,24,4,128]{3,1,2,0:T(8,128)S(1)}, u32[]{:S(2)}, u32[]{:S(2)}) %collective-permute-start.3) | collective-permute-done | bytes 98336 | tf_op jit(solution)/shard_map/ppermute | solution.py:24
  20.1 0.3 fusion.199
  20.4 0.4 copy.45
  20.8 6.6 %collective-permute-start.4 = (f32[2,24,40,4]{2,1,3,0:T(8,128)S(1)}, f32[2,24,40,4]{2,1,3,0:T(8,128)S(1)}, u32[]{:S(2)}, u32[]{:S(2)}) collective-permute-start(f32[2,24,40,4]{2,1,3,0:T(8,128)S(1)} %copy.45), channel_id=1, source_target_pairs={{0,1},{1,2},{2,3},{4,5},{5,6},{6,7},{8,9},{9,10},{10,11},{12,13},{... | collective-permute-start | bytes 92168 | tf_op jit(solution)/shard_map/ppermute | solution.py:22
  27.4 0.4 copy.46
  27.8 1.9 %collective-permute-start.5 = (f32[2,24,40,4]{2,1,3,0:T(8,128)S(1)}, f32[2,24,40,4]{2,1,3,0:T(8,128)S(1)}, u32[]{:S(2)}, u32[]{:S(2)}) collective-permute-start(f32[2,24,40,4]{2,1,3,0:T(8,128)S(1)} %copy.46), channel_id=1, source_target_pairs={{1,0},{2,1},{3,2},{5,4},{6,5},{7,6},{9,8},{10,9},{11,10},{13,12},{... | collective-permute-start | bytes 92168 | tf_op jit(solution)/shard_map/ppermute | solution.py:24
  29.8 0.4 copy.47
  30.2 3.6 %collective-permute-done.5 = f32[2,24,40,4]{2,1,3,0:T(8,128)S(1)} collective-permute-done((f32[2,24,40,4]{2,1,3,0:T(8,128)S(1)}, f32[2,24,40,4]{2,1,3,0:T(8,128)S(1)}, u32[]{:S(2)}, u32[]{:S(2)}) %collective-permute-start.5) | collective-permute-done | bytes 30752 | tf_op jit(solution)/shard_map/ppermute | solution.py:24
  33.7 0.4 copy.48
  34.2 1.0 pad_maximum_fusion.1
  35.2 0.4 slice_bitcast_fusion.1
  35.6 1.8 %pad_maximum_fusion = f32[5,24,40,136]{3,2,1,0:T(8,128)S(1)} fusion(f32[1,24,40,136]{3,2,1,0:T(8,128)S(1)} %get-tuple-element.12, f32[1,24,40,136]{3,2,1,0:T(8,128)S(1)} %get-tuple-element.14, f32[1,24,40,136]{3,2,1,0:T(8,128)S(1)} %get-tuple-element.11, f32[2,24,40,4]{3,2,1,0:T(8,128)S(1)} %copy.48, f32[2,24,4,128]{3,2,1,0:T(4,128)S(1)} %copy.44, ...), kind=kLoop, calls=%fused_computation | loop fusion | flops 4569600 | bytes 5222400 | tf_op jit(solution)/shard_map/stack | solution.py:85
  37.4 3.0 %slice_add_fusion = f32[5,16,40,136]{3,2,1,0:T(8,128)S(1)} fusion(f32[5,24,40,136]{3,2,1,0:T(8,128)S(1)} %pad_maximum_fusion), kind=kLoop, calls=%fused_computation.1 | loop fusion | flops 3481600 | bytes 17408000 | tf_op jit(solution)/shard_map/add | solution.py:59
  40.5 2.0 %slice_add_fusion.8 = f32[5,16,32,136]{3,2,1,0:T(8,128)S(1)} fusion(f32[5,16,40,136]{3,2,1,0:T(8,128)S(1)} %slice_add_fusion), kind=kLoop, calls=%fused_computation.9 | loop fusion | flops 2785280 | bytes 13926400 | tf_op jit(solution)/shard_map/add | solution.py:59
  42.4 2.8 %fusion.4 = f32[5,16,32,128]{3,2,1,0:T(8,128)S(1)} fusion(f32[5,16,32,136]{3,2,1,0:T(8,128)S(1)} %slice_add_fusion.8), kind=kLoop, calls=%fused_computation.25 | loop fusion | flops 2949120 | bytes 13107200 | tf_op jit(solution)/shard_map/div | solution.py:95
  45.2 0.6 fusion.18
  45.8 0.5 multiply_multiply_fusion.1
  46.5 6.2 %fusion = f32[2,3,16,32,20]{3,4,2,1,0:T(8,128)S(1)} fusion(f32[1,3,16,32,128]{4,3,2,1,0:T(8,128)S(1)} %maximum_multiply_fusion.1, f32[1,3,16,32,128]{4,3,2,1,0:T(8,128)S(1)} %maximum_multiply_fusion, f32[20]{0:T(128)S(1)} %multiply_add_fusion), kind=kOutput, calls=%fused_computation.18 | convolution fusion | flops 94806016 | bytes 1818704 | tf_op jit(solution)/shard_map/hcxyz,zk->hcxyk/dot_general | solution.py:127
  52.7 5.9 %convolution_bitcast_fusion.2 = f32[2,3,16,8,20]{4,3,2,1,0:T(8,128)S(1)} fusion(f32[2,3,16,32,20]{3,4,2,1,0:T(8,128)S(1)} %fusion, f32[8]{0:T(128)S(1)} %multiply_add_fusion.1), kind=kOutput, calls=%fused_computation.34 | convolution fusion | flops 5902336 | bytes 307232 | tf_op jit(solution)/shard_map/hcxyk,yj->hcxjk/dot_general | solution.py:128
  58.6 0.4 convolution_bitcast_fusion.3
  59.1 3.2 %collective-permute-start.6 = (f32[2,3,2,8,20]{4,2,3,1,0:T(2,128)S(1)}, f32[2,3,2,8,20]{4,2,3,1,0:T(2,128)S(1)}, u32[]{:S(2)}, u32[]{:S(2)}) collective-permute-start(f32[2,3,2,8,20]{4,2,3,1,0:T(2,128)S(1)} %get-tuple-element.30), channel_id=1, source_target_pairs={{0,8},{8,16},{16,24},{1,9},{9,17},{17,25},{2,10},{10,18},{18,26},{... | collective-permute-start | bytes 23048 | tf_op jit(solution)/shard_map/ppermute | solution.py:22
  62.3 1.5 %collective-permute-start.7 = (f32[2,3,2,8,20]{4,2,3,1,0:T(2,128)S(1)}, f32[2,3,2,8,20]{4,2,3,1,0:T(2,128)S(1)}, u32[]{:S(2)}, u32[]{:S(2)}) collective-permute-start(f32[2,3,2,8,20]{4,2,3,1,0:T(2,128)S(1)} %get-tuple-element.31), channel_id=1, source_target_pairs={{8,0},{16,8},{24,16},{9,1},{17,9},{25,17},{10,2},{18,10},{26,18},{... | collective-permute-start | bytes 23048 | tf_op jit(solution)/shard_map/ppermute | solution.py:24
  63.8 3.3 %collective-permute-done.7 = f32[2,3,2,8,20]{4,2,3,1,0:T(2,128)S(1)} collective-permute-done((f32[2,3,2,8,20]{4,2,3,1,0:T(2,128)S(1)}, f32[2,3,2,8,20]{4,2,3,1,0:T(2,128)S(1)}, u32[]{:S(2)}, u32[]{:S(2)}) %collective-permute-start.7) | collective-permute-done | bytes 7712 | tf_op jit(solution)/shard_map/ppermute | solution.py:24
  67.4 3.3 %collective-permute-start.8 = (f32[2,3,10,8,2]{4,2,3,1,0:T(8,128)S(1)}, f32[2,3,10,8,2]{4,2,3,1,0:T(8,128)S(1)}, u32[]{:S(2)}, u32[]{:S(2)}) collective-permute-start(f32[2,3,10,8,2]{4,2,3,1,0:T(8,128)S(1)} %get-tuple-element.26), channel_id=1, source_target_pairs={{0,1},{1,2},{2,3},{4,5},{5,6},{6,7},{8,9},{9,10},{10,11},{12,13},{... | collective-permute-start | bytes 11528 | tf_op jit(solution)/shard_map/ppermute | solution.py:22
  70.6 1.9 %collective-permute-start.9 = (f32[2,3,10,8,2]{4,2,3,1,0:T(8,128)S(1)}, f32[2,3,10,8,2]{4,2,3,1,0:T(8,128)S(1)}, u32[]{:S(2)}, u32[]{:S(2)}) collective-permute-start(f32[2,3,10,8,2]{4,2,3,1,0:T(8,128)S(1)} %get-tuple-element.27), channel_id=1, source_target_pairs={{1,0},{2,1},{3,2},{5,4},{6,5},{7,6},{9,8},{10,9},{11,10},{13,12},{... | collective-permute-start | bytes 11528 | tf_op jit(solution)/shard_map/ppermute | solution.py:24
  72.6 2.8 %collective-permute-done.8 = f32[2,3,10,8,2]{4,2,3,1,0:T(8,128)S(1)} collective-permute-done((f32[2,3,10,8,2]{4,2,3,1,0:T(8,128)S(1)}, f32[2,3,10,8,2]{4,2,3,1,0:T(8,128)S(1)}, u32[]{:S(2)}, u32[]{:S(2)}) %collective-permute-start.8) | collective-permute-done | bytes 3872 | tf_op jit(solution)/shard_map/ppermute | solution.py:22
  75.3 4.4 %collective-permute-done.9 = f32[2,3,10,8,2]{4,2,3,1,0:T(8,128)S(1)} collective-permute-done((f32[2,3,10,8,2]{4,2,3,1,0:T(8,128)S(1)}, f32[2,3,10,8,2]{4,2,3,1,0:T(8,128)S(1)}, u32[]{:S(2)}, u32[]{:S(2)}) %collective-permute-start.9) | collective-permute-done | bytes 3872 | tf_op jit(solution)/shard_map/ppermute | solution.py:24
  79.8 0.6 convolution_bitcast_fusion.5
  80.6 3.9 %all_gather.7 = f32[2,2,3,2,12,16]{5,3,4,2,1,0:T(2,128)S(1)} all-gather(f32[1,2,3,2,12,16]{5,3,4,2,1,0:T(2,128)S(1)} %copy_dynamic-update-slice_fusion), channel_id=1, replica_groups=mesh['gx'=4,'gy'=2,'gz'=4] {'gy'}, dimensions={0}, use_global_device_ids=true | all-gather | bytes 27648 | tf_op jit(solution)/shard_map/all_gather | solution.py:11
  84.7 3.2 %collective-permute-start.10 = (f32[2,3,2,8,16]{4,2,3,1,0:T(2,128)S(1)}, f32[2,3,2,8,16]{4,2,3,1,0:T(2,128)S(1)}, u32[]{:S(2)}, u32[]{:S(2)}) collective-permute-start(f32[2,3,2,8,16]{4,2,3,1,0:T(2,128)S(1)} %fusion.51), channel_id=1, source_target_pairs={{0,8},{8,16},{16,24},{1,9},{9,17},{17,25},{2,10},{10,18},{18,26},{... | collective-permute-start | bytes 18440 | tf_op jit(solution)/shard_map/ppermute | solution.py:22
  87.9 1.3 %collective-permute-start.11 = (f32[2,3,2,8,16]{4,2,3,1,0:T(2,128)S(1)}, f32[2,3,2,8,16]{4,2,3,1,0:T(2,128)S(1)}, u32[]{:S(2)}, u32[]{:S(2)}) collective-permute-start(f32[2,3,2,8,16]{4,2,3,1,0:T(2,128)S(1)} %fusion.51), channel_id=1, source_target_pairs={{8,0},{16,8},{24,16},{9,1},{17,9},{25,17},{10,2},{18,10},{26,18},{... | collective-permute-start | bytes 18440 | tf_op jit(solution)/shard_map/ppermute | solution.py:24
  89.2 3.5 %collective-permute-done.11 = f32[2,3,2,8,16]{4,2,3,1,0:T(2,128)S(1)} collective-permute-done((f32[2,3,2,8,16]{4,2,3,1,0:T(2,128)S(1)}, f32[2,3,2,8,16]{4,2,3,1,0:T(2,128)S(1)}, u32[]{:S(2)}, u32[]{:S(2)}) %collective-permute-start.11) | collective-permute-done | bytes 6176 | tf_op jit(solution)/shard_map/ppermute | solution.py:24
  92.9 4.3 %collective-permute-start.12 = (f32[2,3,6,8,2]{4,2,3,1,0:T(8,128)S(1)}, f32[2,3,6,8,2]{4,2,3,1,0:T(8,128)S(1)}, u32[]{:S(2)}, u32[]{:S(2)}) collective-permute-start(f32[2,3,6,8,2]{4,2,3,1,0:T(8,128)S(1)} %get-tuple-element.29), channel_id=1, source_target_pairs={{0,1},{1,2},{2,3},{4,5},{5,6},{6,7},{8,9},{9,10},{10,11},{12,13},{... | collective-permute-start | bytes 6920 | tf_op jit(solution)/shard_map/ppermute | solution.py:22
  97.2 1.9 %collective-permute-start.13 = (f32[2,3,6,8,2]{4,2,3,1,0:T(8,128)S(1)}, f32[2,3,6,8,2]{4,2,3,1,0:T(8,128)S(1)}, u32[]{:S(2)}, u32[]{:S(2)}) collective-permute-start(f32[2,3,6,8,2]{4,2,3,1,0:T(8,128)S(1)} %get-tuple-element.28), channel_id=1, source_target_pairs={{1,0},{2,1},{3,2},{5,4},{6,5},{7,6},{9,8},{10,9},{11,10},{13,12},{... | collective-permute-start | bytes 6920 | tf_op jit(solution)/shard_map/ppermute | solution.py:24
  99.2 0.6 copy.54
  99.8 4.4 %collective-permute-done.13 = f32[2,3,6,8,2]{4,2,3,1,0:T(8,128)S(1)} collective-permute-done((f32[2,3,6,8,2]{4,2,3,1,0:T(8,128)S(1)}, f32[2,3,6,8,2]{4,2,3,1,0:T(8,128)S(1)}, u32[]{:S(2)}, u32[]{:S(2)}) %collective-permute-start.13) | collective-permute-done | bytes 2336 | tf_op jit(solution)/shard_map/ppermute | solution.py:24
  104.2 0.9 convolution_bitcast_fusion.1
  105.1 2.1 %convolution_bitcast_fusion = f32[2,3,16,32,20]{3,4,2,1,0:T(8,128)S(1)} fusion(f32[2,3,16,8,20]{4,2,3,1,0:T(8,128)S(1)} %convolution_bitcast_fusion.1, f32[8]{0:T(128)S(1)} %multiply_add_fusion.1), kind=kOutput, calls=%fused_computation.23 | convolution fusion | flops 5902336 | bytes 307232 | tf_op jit(solution)/shard_map/hcxjk,yj->hcxyk/dot_general | solution.py:145
  107.2 3.6 %convolution_convert_fusion = bf16[2,3,16,32,128]{4,3,2,1,0:T(8,128)(2,1)} fusion(f32[2,3,16,32,20]{3,4,2,1,0:T(8,128)S(1)} %convolution_bitcast_fusion, f32[20]{0:T(128)S(1)} %multiply_add_fusion), kind=kOutput, calls=%fused_computation.22 | convolution fusion | flops 94806016 | bytes 1032272 | tf_op jit(solution)/shard_map/hcxyk,zk->hcxyz/dot_general | solution.py:146
  (36 shorter events, 1.5 us)
Async XLA Ops:
  1.6 6.2 %collective-permute-start = (f32[2,4,32,128]{3,2,1,0:T(8,128)S(1)}, f32[2,4,32,128]{3,2,1,0:T(8,128)S(1)}, u32[]{:S(2)}, u32[]{:S(2)}) collective-permute-start(f32[2,4,32,128]{3,2,1,0:T(8,128)S(1)} %get-tuple-element.25), channel_id=1, source_target_pairs={{0,8},{8,16},{16,24},{1,9},{9,17},{17,25},{2,10},{10,18},{18,26},{... | collective-permute-start | bytes 393224 | tf_op jit(solution)/shard_map/ppermute | solution.py:22
  5.7 5.7 %collective-permute-start.1 = (f32[2,4,32,128]{3,2,1,0:T(8,128)S(1)}, f32[2,4,32,128]{3,2,1,0:T(8,128)S(1)}, u32[]{:S(2)}, u32[]{:S(2)}) collective-permute-start(f32[2,4,32,128]{3,2,1,0:T(8,128)S(1)} %get-tuple-element.24), channel_id=1, source_target_pairs={{8,0},{16,8},{24,16},{9,1},{17,9},{25,17},{10,2},{18,10},{26,18},{... | collective-permute-start | bytes 393224 | tf_op jit(solution)/shard_map/ppermute | solution.py:24
  11.4 4.7 %collective-permute-start.2 = (f32[2,24,4,128]{3,1,2,0:T(8,128)S(1)}, f32[2,24,4,128]{3,1,2,0:T(8,128)S(1)}, u32[]{:S(2)}, u32[]{:S(2)}) collective-permute-start(f32[2,24,4,128]{3,1,2,0:T(8,128)S(1)} %copy.60), channel_id=1, source_target_pairs={{0,4},{1,5},{2,6},{3,7},{8,12},{9,13},{10,14},{11,15},{16,20},{17,... | collective-permute-start | bytes 294920 | tf_op jit(solution)/shard_map/ppermute | solution.py:22
  14.6 5.4 %collective-permute-start.3 = (f32[2,24,4,128]{3,1,2,0:T(8,128)S(1)}, f32[2,24,4,128]{3,1,2,0:T(8,128)S(1)}, u32[]{:S(2)}, u32[]{:S(2)}) collective-permute-start(f32[2,24,4,128]{3,1,2,0:T(8,128)S(1)} %copy.61), channel_id=1, source_target_pairs={{4,0},{5,1},{6,2},{7,3},{12,8},{13,9},{14,10},{15,11},{20,16},{21,... | collective-permute-start | bytes 294920 | tf_op jit(solution)/shard_map/ppermute | solution.py:24
  20.8 8.9 %collective-permute-start.4 = (f32[2,24,40,4]{2,1,3,0:T(8,128)S(1)}, f32[2,24,40,4]{2,1,3,0:T(8,128)S(1)}, u32[]{:S(2)}, u32[]{:S(2)}) collective-permute-start(f32[2,24,40,4]{2,1,3,0:T(8,128)S(1)} %copy.45), channel_id=1, source_target_pairs={{0,1},{1,2},{2,3},{4,5},{5,6},{6,7},{8,9},{9,10},{10,11},{12,13},{... | collective-permute-start | bytes 92168 | tf_op jit(solution)/shard_map/ppermute | solution.py:22
  27.8 5.9 %collective-permute-start.5 = (f32[2,24,40,4]{2,1,3,0:T(8,128)S(1)}, f32[2,24,40,4]{2,1,3,0:T(8,128)S(1)}, u32[]{:S(2)}, u32[]{:S(2)}) collective-permute-start(f32[2,24,40,4]{2,1,3,0:T(8,128)S(1)} %copy.46), channel_id=1, source_target_pairs={{1,0},{2,1},{3,2},{5,4},{6,5},{7,6},{9,8},{10,9},{11,10},{13,12},{... | collective-permute-start | bytes 92168 | tf_op jit(solution)/shard_map/ppermute | solution.py:24
  58.6 26.0 %copy-start = (f32[2,3,2,8,16]{4,3,2,1,0:T(8,128)S(1)}, f32[2,3,2,8,16]{4,3,2,1,0:T(8,128)}, u32[]{:S(2)}) copy-start(f32[2,3,2,8,16]{4,3,2,1,0:T(8,128)} %param.3) | copy-start | bytes 18436
  59.1 4.7 %collective-permute-start.6 = (f32[2,3,2,8,20]{4,2,3,1,0:T(2,128)S(1)}, f32[2,3,2,8,20]{4,2,3,1,0:T(2,128)S(1)}, u32[]{:S(2)}, u32[]{:S(2)}) collective-permute-start(f32[2,3,2,8,20]{4,2,3,1,0:T(2,128)S(1)} %get-tuple-element.30), channel_id=1, source_target_pairs={{0,8},{8,16},{16,24},{1,9},{9,17},{17,25},{2,10},{10,18},{18,26},{... | collective-permute-start | bytes 23048 | tf_op jit(solution)/shard_map/ppermute | solution.py:22
  62.3 4.8 %collective-permute-start.7 = (f32[2,3,2,8,20]{4,2,3,1,0:T(2,128)S(1)}, f32[2,3,2,8,20]{4,2,3,1,0:T(2,128)S(1)}, u32[]{:S(2)}, u32[]{:S(2)}) collective-permute-start(f32[2,3,2,8,20]{4,2,3,1,0:T(2,128)S(1)} %get-tuple-element.31), channel_id=1, source_target_pairs={{8,0},{16,8},{24,16},{9,1},{17,9},{25,17},{10,2},{18,10},{26,18},{... | collective-permute-start | bytes 23048 | tf_op jit(solution)/shard_map/ppermute | solution.py:24
  67.4 8.0 %collective-permute-start.8 = (f32[2,3,10,8,2]{4,2,3,1,0:T(8,128)S(1)}, f32[2,3,10,8,2]{4,2,3,1,0:T(8,128)S(1)}, u32[]{:S(2)}, u32[]{:S(2)}) collective-permute-start(f32[2,3,10,8,2]{4,2,3,1,0:T(8,128)S(1)} %get-tuple-element.26), channel_id=1, source_target_pairs={{0,1},{1,2},{2,3},{4,5},{5,6},{6,7},{8,9},{9,10},{10,11},{12,13},{... | collective-permute-start | bytes 11528 | tf_op jit(solution)/shard_map/ppermute | solution.py:22
  70.6 9.1 %collective-permute-start.9 = (f32[2,3,10,8,2]{4,2,3,1,0:T(8,128)S(1)}, f32[2,3,10,8,2]{4,2,3,1,0:T(8,128)S(1)}, u32[]{:S(2)}, u32[]{:S(2)}) collective-permute-start(f32[2,3,10,8,2]{4,2,3,1,0:T(8,128)S(1)} %get-tuple-element.27), channel_id=1, source_target_pairs={{1,0},{2,1},{3,2},{5,4},{6,5},{7,6},{9,8},{10,9},{11,10},{13,12},{... | collective-permute-start | bytes 11528 | tf_op jit(solution)/shard_map/ppermute | solution.py:24
  84.7 4.5 %collective-permute-start.10 = (f32[2,3,2,8,16]{4,2,3,1,0:T(2,128)S(1)}, f32[2,3,2,8,16]{4,2,3,1,0:T(2,128)S(1)}, u32[]{:S(2)}, u32[]{:S(2)}) collective-permute-start(f32[2,3,2,8,16]{4,2,3,1,0:T(2,128)S(1)} %fusion.51), channel_id=1, source_target_pairs={{0,8},{8,16},{16,24},{1,9},{9,17},{17,25},{2,10},{10,18},{18,26},{... | collective-permute-start | bytes 18440 | tf_op jit(solution)/shard_map/ppermute | solution.py:22
  87.9 4.8 %collective-permute-start.11 = (f32[2,3,2,8,16]{4,2,3,1,0:T(2,128)S(1)}, f32[2,3,2,8,16]{4,2,3,1,0:T(2,128)S(1)}, u32[]{:S(2)}, u32[]{:S(2)}) collective-permute-start(f32[2,3,2,8,16]{4,2,3,1,0:T(2,128)S(1)} %fusion.51), channel_id=1, source_target_pairs={{8,0},{16,8},{24,16},{9,1},{17,9},{25,17},{10,2},{18,10},{26,18},{... | collective-permute-start | bytes 18440 | tf_op jit(solution)/shard_map/ppermute | solution.py:24
  92.9 6.9 %collective-permute-start.12 = (f32[2,3,6,8,2]{4,2,3,1,0:T(8,128)S(1)}, f32[2,3,6,8,2]{4,2,3,1,0:T(8,128)S(1)}, u32[]{:S(2)}, u32[]{:S(2)}) collective-permute-start(f32[2,3,6,8,2]{4,2,3,1,0:T(8,128)S(1)} %get-tuple-element.29), channel_id=1, source_target_pairs={{0,1},{1,2},{2,3},{4,5},{5,6},{6,7},{8,9},{9,10},{10,11},{12,13},{... | collective-permute-start | bytes 6920 | tf_op jit(solution)/shard_map/ppermute | solution.py:22
  97.2 7.0 %collective-permute-start.13 = (f32[2,3,6,8,2]{4,2,3,1,0:T(8,128)S(1)}, f32[2,3,6,8,2]{4,2,3,1,0:T(8,128)S(1)}, u32[]{:S(2)}, u32[]{:S(2)}) collective-permute-start(f32[2,3,6,8,2]{4,2,3,1,0:T(8,128)S(1)} %get-tuple-element.28), channel_id=1, source_target_pairs={{1,0},{2,1},{3,2},{5,4},{6,5},{7,6},{9,8},{10,9},{11,10},{13,12},{... | collective-permute-start | bytes 6920 | tf_op jit(solution)/shard_map/ppermute | solution.py:24
